TPU v7x, 256 devices: a whole 4x4x8 slice. The times are simulated.
256 devices in a mesh: gx: 16 (over z, core), gy: 16 (over x, y).
Axes of the slice: x: 4, y: 4, z: 8, core: 2. Of those that a mesh axis runs over, the one named last changes fastest.
Arguments:
- density: float32 [256, 256, 128], P('gx', 'gy'), may hold values from 0.05 to 40, as said below
Outputs:
- potential: float32 [256, 256, 128], P('gx', 'gy')
Inputs may be any that keep to these rules, and one draw needn't show every extreme that they name: `density`: densities are positive.
All inputs are finite; a program needn't handle non-finite values.
Results may differ from a plain program's by a relative error of at most 0.00014.
Values sent between devices are 32-bit elements; how exact they have to be, the bound alone decides.
A program may use at most 64 MiB of HBM per device.

v0:
```python
import jax
import jax.numpy as jnp
from jax import lax
from jax.sharding import Mesh
from jax.sharding import PartitionSpec as P

LEVELS = 4
NEWTON = 3
GX_GY = ("gx_0", "gx_1", "gy_0", "gy_1")
GX = ("gx_0", "gx_1")
GY = ("gy_0", "gy_1")
COUPLING = 0.1
FLOOR = 3.0


def extended(x, sides, width):
    for axis, dim in sides:
        peers, length = (lax.axis_size(axis), x.shape[dim])
        up = [(i, (i + 1) % peers) for i in range(peers)]
        down = [(j, i) for i, j in up]
        last = lax.slice_in_dim(x, length - width, length, axis=dim)
        leading = lax.slice_in_dim(x, 0, width, axis=dim)
        before = lax.ppermute(last, axis, up)
        after = lax.ppermute(leading, axis, down)
        x = jnp.concatenate([before, x, after], axis=dim)
    return x


def one_axis_at_a_time(x, axes):
    for axis in axes:
        x = lax.psum(x, axis)
    return x


def shifted(padded, off_x, off_y, off_z):
    size_x = padded.shape[0] - 2
    size_y = padded.shape[1] - 2
    size_z = padded.shape[2] - 2
    return padded[
        1 + off_x : 1 + off_x + size_x,
        1 + off_y : 1 + off_y + size_y,
        1 + off_z : 1 + off_z + size_z,
    ]


def hessian(padded, spacing_inv):
    center = shifted(padded, 0, 0, 0)
    pure_x = (shifted(padded, 1, 0, 0) + shifted(padded, -1, 0, 0) - 2.0 * center) * spacing_inv
    pure_y = (shifted(padded, 0, 1, 0) + shifted(padded, 0, -1, 0) - 2.0 * center) * spacing_inv
    pure_z = (shifted(padded, 0, 0, 1) + shifted(padded, 0, 0, -1) - 2.0 * center) * spacing_inv
    quarter = 0.25 * spacing_inv
    mixed_xy = (
        shifted(padded, 1, 1, 0)
        - shifted(padded, 1, -1, 0)
        - shifted(padded, -1, 1, 0)
        + shifted(padded, -1, -1, 0)
    ) * quarter
    mixed_xz = (
        shifted(padded, 1, 0, 1)
        - shifted(padded, 1, 0, -1)
        - shifted(padded, -1, 0, 1)
        + shifted(padded, -1, 0, -1)
    ) * quarter
    mixed_yz = (
        shifted(padded, 0, 1, 1)
        - shifted(padded, 0, 1, -1)
        - shifted(padded, 0, -1, 1)
        + shifted(padded, 0, -1, -1)
    ) * quarter
    return (pure_x, pure_y, pure_z, mixed_xy, mixed_xz, mixed_yz)


def nonlinear(padded, source):
    pure_x, pure_y, pure_z, mixed_xy, mixed_xz, mixed_yz = hessian(padded, 1.0)
    cubic = 2.0 * (
        pure_x * pure_y
        + pure_x * pure_z
        + pure_y * pure_z
        - mixed_xy * mixed_xy
        - mixed_xz * mixed_xz
        - mixed_yz * mixed_yz
    )
    return pure_x + pure_y + pure_z + COUPLING * cubic - source


def coefficients(padded, spacing_inv):
    pure_x, pure_y, pure_z, mixed_xy, mixed_xz, mixed_yz = hessian(padded, spacing_inv)
    stiff_x = 1.0 + 2.0 * COUPLING * (pure_y + pure_z)
    stiff_y = 1.0 + 2.0 * COUPLING * (pure_x + pure_z)
    stiff_z = 1.0 + 2.0 * COUPLING * (pure_x + pure_y)
    diagonal = jnp.maximum(2.0 * (stiff_x + stiff_y + stiff_z), FLOOR)
    relax = 1.0 / (spacing_inv * diagonal)
    return jnp.stack(
        [
            stiff_x,
            stiff_y,
            stiff_z,
            -4.0 * COUPLING * mixed_xy,
            -4.0 * COUPLING * mixed_xz,
            -4.0 * COUPLING * mixed_yz,
            relax,
        ]
    )


def jacobian(padded, weights, spacing_inv):
    parts = hessian(padded, spacing_inv)
    result = weights[0] * parts[0]
    for index in range(1, 6):
        result = result + weights[index] * parts[index]
    return result


def restrict(field):
    size_x, size_y, size_z = field.shape
    blocks = field.reshape(size_x // 2, 2, size_y // 2, 2, size_z // 2, 2)
    return jnp.sum(blocks, axis=(1, 3, 5)) * 0.125


def prolong(field):
    size_x, size_y, size_z = field.shape
    spread = jnp.broadcast_to(field[:, None, :, None, :, None], (size_x, 2, size_y, 2, size_z, 2))
    return spread.reshape(2 * size_x, 2 * size_y, 2 * size_z)


def wrap_depth(field):
    return jnp.concatenate([field[..., -1:], field, field[..., :1]], axis=-1)


def extend(field):
    return wrap_depth(extended(field, ((GX, 0), (GY, 1)), 1))


def checker(shape, first_x, first_y, first_z):
    index_x = first_x + jnp.arange(shape[0], dtype=jnp.int32)
    index_y = first_y + jnp.arange(shape[1], dtype=jnp.int32)
    index_z = first_z + jnp.arange(shape[2], dtype=jnp.int32)
    parity = (index_x[:, None, None] + index_y[None, :, None] + index_z[None, None, :]) % 2
    return (parity == 0).astype(jnp.float32)


def black_half(change, target, weights, red_mask, pad_field, spacing_inv):
    black_mask = 1.0 - red_mask
    return (
        change
        + black_mask * (jacobian(pad_field(change), weights, spacing_inv) - target) * weights[6]
    )


def first_sweep(target, weights, red_mask, pad_field, spacing_inv):
    change = -red_mask * target * weights[6]
    return black_half(change, target, weights, red_mask, pad_field, spacing_inv)


def full_sweep(change, target, weights, red_mask, pad_field, spacing_inv):
    change = (
        change
        + red_mask * (jacobian(pad_field(change), weights, spacing_inv) - target) * weights[6]
    )
    return black_half(change, target, weights, red_mask, pad_field, spacing_inv)


def edge_terms():
    return None


def start_sweep(target, context):
    weights, red_mask, spacing_inv, wide = context
    return first_sweep(target, weights, red_mask, extend, spacing_inv)


def more_sweep(change, target, context):
    weights, red_mask, spacing_inv, wide = context
    return full_sweep(change, target, weights, red_mask, extend, spacing_inv)


def cycle(coarse_level, target, weight_levels, mask_levels, wide_masks):
    spacing_inv = 0.25**coarse_level
    weights = weight_levels[coarse_level]
    red_mask = mask_levels[coarse_level]
    context = (weights, red_mask, spacing_inv, edge_terms())
    change = start_sweep(target, context)
    if coarse_level == LEVELS - 1:
        change = more_sweep(change, target, context)
        return change
    leftover = target - jacobian(extend(change), weights, spacing_inv)
    change = change + prolong(
        cycle(coarse_level + 1, restrict(leftover), weight_levels, mask_levels, wide_masks)
    )
    return more_sweep(change, target, context)


def per_device(density):
    cells_total = float(density.size * lax.axis_size(GX) * lax.axis_size(GY))
    mass_total = one_axis_at_a_time(jnp.sum(density), GX_GY)
    source = density / (mass_total / cells_total) - 1.0
    mask_levels = []
    wide_masks = []
    for coarse_level in range(LEVELS):
        shape = (
            density.shape[0] >> coarse_level,
            density.shape[1] >> coarse_level,
            density.shape[2] >> coarse_level,
        )
        start_x = lax.axis_index(GX) * shape[0]
        start_y = lax.axis_index(GY) * shape[1]
        mask_levels.append(checker(shape, start_x, start_y, 0))
        wide_shape = (shape[0] + 2, shape[1] + 2, shape[2] + 2)
        wide_masks.append(checker(wide_shape, start_x - 1, start_y - 1, -1))

    def newton_turn(newton_step, potential):
        padded_levels = []
        coarse = potential
        for coarse_level in range(LEVELS):
            if coarse_level > 0:
                coarse = restrict(coarse)
            padded_levels.append(extend(coarse))
        weight_levels = [
            coefficients(padded_levels[coarse_level], 0.25**coarse_level)
            for coarse_level in range(LEVELS)
        ]
        target = -nonlinear(padded_levels[0], source)
        return potential + cycle(0, target, weight_levels, mask_levels, wide_masks)

    return lax.fori_loop(0, NEWTON, newton_turn, jnp.zeros_like(density))


def solution(mesh):
    torus = Mesh(mesh.devices.reshape(8, 2, 4, 4), ("gx_0", "gx_1", "gy_0", "gy_1"))
    placed = (P(GX, GY, None),)
    return jax.shard_map(
        per_device, mesh=torus, in_specs=placed, out_specs=P(GX, GY, None), check_vma=False
    )
```

profile of v0, /device:TPU:0, one launch (start us, length us, event | category | flops | bytes accessed | tf_op | source)
XLA Modules:
  0.0 816.9 jit_solution(15661478614758730707)
XLA Ops:
  1.6 19.0 %psum.28 = f32[]{:T(128)} all-reduce(f32[]{:T(128)} %reduce_sum.87), channel_id=1, replica_groups=mesh['gx_0'=8,'gx_1'=2,'gy_0'=4,'gy_1'=4] {'gx_0'}, use_global_device_ids=true, to_apply=%region_1.0 | all-reduce | flops 1 | bytes 8 | tf_op jit(solution)/shard_map/psum | solution.py:31
  23.7 11.2 %psum.30 = f32[]{:T(128)} all-reduce(f32[]{:T(128)} %psum.29), channel_id=1, replica_groups=mesh['gx_0'=8,'gx_1'=2,'gy_0'=4,'gy_1'=4] {'gy_0'}, use_global_device_ids=true, to_apply=%region_3.0 | all-reduce | flops 1 | bytes 8 | tf_op jit(solution)/shard_map/psum | solution.py:31
  34.9 11.4 %psum.31 = f32[]{:T(128)} all-reduce(f32[]{:T(128)} %psum.30), channel_id=1, replica_groups=mesh['gx_0'=8,'gx_1'=2,'gy_0'=4,'gy_1'=4] {'gy_1'}, use_global_device_ids=true, to_apply=%region_4.0 | all-reduce | flops 1 | bytes 8 | tf_op jit(solution)/shard_map/psum | solution.py:31
  48.2 767.6 %while.16 = (s32[]{:T(128)}, f32[16,16,128]{2,1,0:T(8,128)S(1)}, f32[16,16,128]{2,1,0:T(8,128)S(1)}, s32[16,16]{1,0:T(8,128)S(1)}, s32[8,8]{1,0:T(8,128)S(1)}, /...) while((s32[]{:T(128)}, f32[16,16,128]{2,1,0:T(8,128)S(1)}, ...), condition=%wide.region_12.13_spmd.clone.clone.clone, body=%wide.region_5.12_spmd.clone.clone.clone.sunk | while | flops 16104283 | bytes 31824424 | solution.py:225
  49.2 9.8 %reshape.257 = f32[8,2,8,2,64,2]{5,4,3,2,1,0:T(8,128)} reshape(f32[16,16,128]{2,1,0:T(8,128)S(1)} %broadcast_select_fusion.2) | data formatting | bytes 262144 | tf_op jit(solution)/shard_map/while/body/eval_jaxpr/reshape | solution.py:116
  59.0 4.0 reduce_sum.113
  75.5 5.4 collective-permute-start.39
  89.5 5.7 collective-permute-done.15
  95.2 4.2 collective-permute-done.5
  120.0 9.8 %reshape.256 = f32[8,2,8,2,64,2]{5,4,3,2,1,0:T(8,128)} reshape(f32[16,16,128]{2,1,0:T(8,128)S(1)} %fusion.546) | data formatting | bytes 262144 | tf_op jit(solution)/shard_map/while/body/eval_jaxpr/reshape | solution.py:116
  129.8 4.0 reduce_sum.112
  142.0 5.3 collective-permute-done.19
  268.2 4.0 broadcast_in_dim.60
  272.2 6.9 reshape.262
  304.6 9.8 %reshape.257 = f32[8,2,8,2,64,2]{5,4,3,2,1,0:T(8,128)} reshape(f32[16,16,128]{2,1,0:T(8,128)S(1)} %broadcast_select_fusion.2) | data formatting | bytes 262144 | tf_op jit(solution)/shard_map/while/body/eval_jaxpr/reshape | solution.py:116
  314.4 4.0 reduce_sum.113
  330.9 5.4 collective-permute-start.39
  344.9 5.7 collective-permute-done.15
  350.6 4.2 collective-permute-done.5
  375.6 9.8 %reshape.256 = f32[8,2,8,2,64,2]{5,4,3,2,1,0:T(8,128)} reshape(f32[16,16,128]{2,1,0:T(8,128)S(1)} %fusion.546) | data formatting | bytes 262144 | tf_op jit(solution)/shard_map/while/body/eval_jaxpr/reshape | solution.py:116
  385.4 4.0 reduce_sum.112
  397.6 5.3 collective-permute-done.19
  527.5 6.9 reshape.262
  560.2 9.8 %reshape.257 = f32[8,2,8,2,64,2]{5,4,3,2,1,0:T(8,128)} reshape(f32[16,16,128]{2,1,0:T(8,128)S(1)} %broadcast_select_fusion.2) | data formatting | bytes 262144 | tf_op jit(solution)/shard_map/while/body/eval_jaxpr/reshape | solution.py:116
  570.0 4.0 reduce_sum.113
  586.5 5.4 collective-permute-start.39
  600.5 5.7 collective-permute-done.15
  606.2 4.2 collective-permute-done.5
  631.0 9.8 %reshape.256 = f32[8,2,8,2,64,2]{5,4,3,2,1,0:T(8,128)} reshape(f32[16,16,128]{2,1,0:T(8,128)S(1)} %fusion.546) | data formatting | bytes 262144 | tf_op jit(solution)/shard_map/while/body/eval_jaxpr/reshape | solution.py:116
  640.8 4.0 reduce_sum.112
  653.0 5.3 collective-permute-done.19
  783.1 6.9 reshape.262
  (922 shorter events, 599.7 us)
Async XLA Ops:
  48.7 26.8 %collective-permute-start = (f32[1,16,128]{2,1,0:T(8,128)S(1)}, f32[1,16,128]{2,1,0:T(8,128)S(1)}, u32[]{:S(2)}, u32[]{:S(2)}) collective-permute-start(f32[1,16,128]{2,1,0:T(8,128)S(1)} %get-tuple-element.774), channel_id=1, source_target_pairs={{16,0},{32,16},{48,32},{64,48},{80,64},{96,80},{112,96},{128,112},... | collective-permute-start | bytes 24584 | tf_op jit(solution)/shard_map/while/body/eval_jaxpr/ppermute | solution.py:24
  48.7 32.2 %collective-permute-start.1 = (f32[1,16,128]{2,1,0:T(8,128)S(1)}, f32[1,16,128]{2,1,0:T(8,128)S(1)}, u32[]{:S(2)}, u32[]{:S(2)}) collective-permute-start(f32[1,16,128]{2,1,0:T(8,128)S(1)} %get-tuple-element.775), channel_id=1, source_target_pairs={{0,16},{16,32},{32,48},{48,64},{64,80},{80,96},{96,112},{112,128},... | collective-permute-start | bytes 24584 | tf_op jit(solution)/shard_map/while/body/eval_jaxpr/ppermute | solution.py:23
  63.1 18.0 %collective-permute-start.12 = (f32[1,8,64]{2,1,0:T(8,128)S(1)}, f32[1,8,64]{2,1,0:T(8,128)S(1)}, u32[]{:S(2)}, u32[]{:S(2)}) collective-permute-start(f32[1,8,64]{2,1,0:T(8,128)S(1)} %get-tuple-element.814), channel_id=1, source_target_pairs={{16,0},{32,16},{48,32},{64,48},{80,64},{96,80},{112,96},{128,112},... | collective-permute-start | bytes 6152 | tf_op jit(solution)/shard_map/while/body/eval_jaxpr/ppermute | solution.py:24
  72.6 8.6 %collective-permute-start.13 = (f32[1,8,64]{2,1,0:T(8,128)S(1)}, f32[1,8,64]{2,1,0:T(8,128)S(1)}, u32[]{:S(2)}, u32[]{:S(2)}) collective-permute-start(f32[1,8,64]{2,1,0:T(8,128)S(1)} %get-tuple-element.815), channel_id=1, source_target_pairs={{0,16},{16,32},{32,48},{48,64},{64,80},{80,96},{96,112},{112,128},... | collective-permute-start | bytes 6152 | tf_op jit(solution)/shard_map/while/body/eval_jaxpr/ppermute | solution.py:23
  75.5 85.9 %collective-permute-start.38 = (f32[4,1,16]{2,1,0:T(1,128)S(1)}, f32[4,1,16]{2,1,0:T(1,128)S(1)}, u32[]{:S(2)}, u32[]{:S(2)}) collective-permute-start(f32[4,1,16]{2,1,0:T(1,128)S(1)} %get-tuple-element.892), channel_id=1, source_target_pairs={{0,1},{1,2},{2,3},{3,4},{4,5},{5,6},{6,7},{7,8},{8,9},{9,10},{10,1... | collective-permute-start | bytes 776 | tf_op jit(solution)/shard_map/while/body/eval_jaxpr/ppermute | solution.py:23
  75.5 85.9 %collective-permute-start.39 = (f32[4,1,16]{2,1,0:T(1,128)S(1)}, f32[4,1,16]{2,1,0:T(1,128)S(1)}, u32[]{:S(2)}, u32[]{:S(2)}) collective-permute-start(f32[4,1,16]{2,1,0:T(1,128)S(1)} %get-tuple-element.893), channel_id=1, source_target_pairs={{1,0},{2,1},{3,2},{4,3},{5,4},{6,5},{7,6},{8,7},{9,8},{10,9},{11,1... | collective-permute-start | bytes 776 | tf_op jit(solution)/shard_map/while/body/eval_jaxpr/ppermute | solution.py:24
  81.0 53.0 %collective-permute-start.26 = (f32[6,1,32]{2,1,0:T(1,128)S(1)}, f32[6,1,32]{2,1,0:T(1,128)S(1)}, u32[]{:S(2)}, u32[]{:S(2)}) collective-permute-start(f32[6,1,32]{2,1,0:T(1,128)S(1)} %get-tuple-element.854), channel_id=1, source_target_pairs={{1,0},{2,1},{3,2},{4,3},{5,4},{6,5},{7,6},{8,7},{9,8},{10,9},{11,1... | collective-permute-start | bytes 2312 | tf_op jit(solution)/shard_map/while/body/eval_jaxpr/ppermute | solution.py:24
  81.2 7.1 collective-permute-start.3
  99.6 7.1 collective-permute-start.7
  112.1 7.1 collective-permute-start.11
  115.8 18.7 %collective-permute-start.27 = (f32[6,1,32]{2,1,0:T(1,128)S(1)}, f32[6,1,32]{2,1,0:T(1,128)S(1)}, u32[]{:S(2)}, u32[]{:S(2)}) collective-permute-start(f32[6,1,32]{2,1,0:T(1,128)S(1)} %get-tuple-element.855), channel_id=1, source_target_pairs={{0,1},{1,2},{2,3},{3,4},{4,5},{5,6},{6,7},{7,8},{8,9},{9,10},{10,1... | collective-permute-start | bytes 2312 | tf_op jit(solution)/shard_map/while/body/eval_jaxpr/ppermute | solution.py:23
  176.9 7.2 collective-permute-start.35
  304.1 26.8 %collective-permute-start = (f32[1,16,128]{2,1,0:T(8,128)S(1)}, f32[1,16,128]{2,1,0:T(8,128)S(1)}, u32[]{:S(2)}, u32[]{:S(2)}) collective-permute-start(f32[1,16,128]{2,1,0:T(8,128)S(1)} %get-tuple-element.774), channel_id=1, source_target_pairs={{16,0},{32,16},{48,32},{64,48},{80,64},{96,80},{112,96},{128,112},... | collective-permute-start | bytes 24584 | tf_op jit(solution)/shard_map/while/body/eval_jaxpr/ppermute | solution.py:24
  304.1 32.2 %collective-permute-start.1 = (f32[1,16,128]{2,1,0:T(8,128)S(1)}, f32[1,16,128]{2,1,0:T(8,128)S(1)}, u32[]{:S(2)}, u32[]{:S(2)}) collective-permute-start(f32[1,16,128]{2,1,0:T(8,128)S(1)} %get-tuple-element.775), channel_id=1, source_target_pairs={{0,16},{16,32},{32,48},{48,64},{64,80},{80,96},{96,112},{112,128},... | collective-permute-start | bytes 24584 | tf_op jit(solution)/shard_map/while/body/eval_jaxpr/ppermute | solution.py:23
  318.4 18.0 %collective-permute-start.12 = (f32[1,8,64]{2,1,0:T(8,128)S(1)}, f32[1,8,64]{2,1,0:T(8,128)S(1)}, u32[]{:S(2)}, u32[]{:S(2)}) collective-permute-start(f32[1,8,64]{2,1,0:T(8,128)S(1)} %get-tuple-element.814), channel_id=1, source_target_pairs={{16,0},{32,16},{48,32},{64,48},{80,64},{96,80},{112,96},{128,112},... | collective-permute-start | bytes 6152 | tf_op jit(solution)/shard_map/while/body/eval_jaxpr/ppermute | solution.py:24
  328.0 8.6 %collective-permute-start.13 = (f32[1,8,64]{2,1,0:T(8,128)S(1)}, f32[1,8,64]{2,1,0:T(8,128)S(1)}, u32[]{:S(2)}, u32[]{:S(2)}) collective-permute-start(f32[1,8,64]{2,1,0:T(8,128)S(1)} %get-tuple-element.815), channel_id=1, source_target_pairs={{0,16},{16,32},{32,48},{48,64},{64,80},{80,96},{96,112},{112,128},... | collective-permute-start | bytes 6152 | tf_op jit(solution)/shard_map/while/body/eval_jaxpr/ppermute | solution.py:23
  330.9 86.1 %collective-permute-start.38 = (f32[4,1,16]{2,1,0:T(1,128)S(1)}, f32[4,1,16]{2,1,0:T(1,128)S(1)}, u32[]{:S(2)}, u32[]{:S(2)}) collective-permute-start(f32[4,1,16]{2,1,0:T(1,128)S(1)} %get-tuple-element.892), channel_id=1, source_target_pairs={{0,1},{1,2},{2,3},{3,4},{4,5},{5,6},{6,7},{7,8},{8,9},{9,10},{10,1... | collective-permute-start | bytes 776 | tf_op jit(solution)/shard_map/while/body/eval_jaxpr/ppermute | solution.py:23
  330.9 86.1 %collective-permute-start.39 = (f32[4,1,16]{2,1,0:T(1,128)S(1)}, f32[4,1,16]{2,1,0:T(1,128)S(1)}, u32[]{:S(2)}, u32[]{:S(2)}) collective-permute-start(f32[4,1,16]{2,1,0:T(1,128)S(1)} %get-tuple-element.893), channel_id=1, source_target_pairs={{1,0},{2,1},{3,2},{4,3},{5,4},{6,5},{7,6},{8,7},{9,8},{10,9},{11,1... | collective-permute-start | bytes 776 | tf_op jit(solution)/shard_map/while/body/eval_jaxpr/ppermute | solution.py:24
  336.3 53.3 %collective-permute-start.26 = (f32[6,1,32]{2,1,0:T(1,128)S(1)}, f32[6,1,32]{2,1,0:T(1,128)S(1)}, u32[]{:S(2)}, u32[]{:S(2)}) collective-permute-start(f32[6,1,32]{2,1,0:T(1,128)S(1)} %get-tuple-element.854), channel_id=1, source_target_pairs={{1,0},{2,1},{3,2},{4,3},{5,4},{6,5},{7,6},{8,7},{9,8},{10,9},{11,1... | collective-permute-start | bytes 2312 | tf_op jit(solution)/shard_map/while/body/eval_jaxpr/ppermute | solution.py:24
  355.0 7.1 collective-permute-start.7
  371.4 18.7 %collective-permute-start.27 = (f32[6,1,32]{2,1,0:T(1,128)S(1)}, f32[6,1,32]{2,1,0:T(1,128)S(1)}, u32[]{:S(2)}, u32[]{:S(2)}) collective-permute-start(f32[6,1,32]{2,1,0:T(1,128)S(1)} %get-tuple-element.855), channel_id=1, source_target_pairs={{0,1},{1,2},{2,3},{3,4},{4,5},{5,6},{6,7},{7,8},{8,9},{9,10},{10,1... | collective-permute-start | bytes 2312 | tf_op jit(solution)/shard_map/while/body/eval_jaxpr/ppermute | solution.py:23
  432.6 7.2 collective-permute-start.35
  538.9 7.1 collective-permute-start.71
  559.7 26.8 %collective-permute-start = (f32[1,16,128]{2,1,0:T(8,128)S(1)}, f32[1,16,128]{2,1,0:T(8,128)S(1)}, u32[]{:S(2)}, u32[]{:S(2)}) collective-permute-start(f32[1,16,128]{2,1,0:T(8,128)S(1)} %get-tuple-element.774), channel_id=1, source_target_pairs={{16,0},{32,16},{48,32},{64,48},{80,64},{96,80},{112,96},{128,112},... | collective-permute-start | bytes 24584 | tf_op jit(solution)/shard_map/while/body/eval_jaxpr/ppermute | solution.py:24
  559.7 32.2 %collective-permute-start.1 = (f32[1,16,128]{2,1,0:T(8,128)S(1)}, f32[1,16,128]{2,1,0:T(8,128)S(1)}, u32[]{:S(2)}, u32[]{:S(2)}) collective-permute-start(f32[1,16,128]{2,1,0:T(8,128)S(1)} %get-tuple-element.775), channel_id=1, source_target_pairs={{0,16},{16,32},{32,48},{48,64},{64,80},{80,96},{96,112},{112,128},... | collective-permute-start | bytes 24584 | tf_op jit(solution)/shard_map/while/body/eval_jaxpr/ppermute | solution.py:23
  574.1 18.0 %collective-permute-start.12 = (f32[1,8,64]{2,1,0:T(8,128)S(1)}, f32[1,8,64]{2,1,0:T(8,128)S(1)}, u32[]{:S(2)}, u32[]{:S(2)}) collective-permute-start(f32[1,8,64]{2,1,0:T(8,128)S(1)} %get-tuple-element.814), channel_id=1, source_target_pairs={{16,0},{32,16},{48,32},{64,48},{80,64},{96,80},{112,96},{128,112},... | collective-permute-start | bytes 6152 | tf_op jit(solution)/shard_map/while/body/eval_jaxpr/ppermute | solution.py:24
  583.6 8.6 %collective-permute-start.13 = (f32[1,8,64]{2,1,0:T(8,128)S(1)}, f32[1,8,64]{2,1,0:T(8,128)S(1)}, u32[]{:S(2)}, u32[]{:S(2)}) collective-permute-start(f32[1,8,64]{2,1,0:T(8,128)S(1)} %get-tuple-element.815), channel_id=1, source_target_pairs={{0,16},{16,32},{32,48},{48,64},{64,80},{80,96},{96,112},{112,128},... | collective-permute-start | bytes 6152 | tf_op jit(solution)/shard_map/while/body/eval_jaxpr/ppermute | solution.py:23
  586.5 85.9 %collective-permute-start.38 = (f32[4,1,16]{2,1,0:T(1,128)S(1)}, f32[4,1,16]{2,1,0:T(1,128)S(1)}, u32[]{:S(2)}, u32[]{:S(2)}) collective-permute-start(f32[4,1,16]{2,1,0:T(1,128)S(1)} %get-tuple-element.892), channel_id=1, source_target_pairs={{0,1},{1,2},{2,3},{3,4},{4,5},{5,6},{6,7},{7,8},{8,9},{9,10},{10,1... | collective-permute-start | bytes 776 | tf_op jit(solution)/shard_map/while/body/eval_jaxpr/ppermute | solution.py:23
  586.5 85.9 %collective-permute-start.39 = (f32[4,1,16]{2,1,0:T(1,128)S(1)}, f32[4,1,16]{2,1,0:T(1,128)S(1)}, u32[]{:S(2)}, u32[]{:S(2)}) collective-permute-start(f32[4,1,16]{2,1,0:T(1,128)S(1)} %get-tuple-element.893), channel_id=1, source_target_pairs={{1,0},{2,1},{3,2},{4,3},{5,4},{6,5},{7,6},{8,7},{9,8},{10,9},{11,1... | collective-permute-start | bytes 776 | tf_op jit(solution)/shard_map/while/body/eval_jaxpr/ppermute | solution.py:24
  591.9 53.0 %collective-permute-start.26 = (f32[6,1,32]{2,1,0:T(1,128)S(1)}, f32[6,1,32]{2,1,0:T(1,128)S(1)}, u32[]{:S(2)}, u32[]{:S(2)}) collective-permute-start(f32[6,1,32]{2,1,0:T(1,128)S(1)} %get-tuple-element.854), channel_id=1, source_target_pairs={{1,0},{2,1},{3,2},{4,3},{5,4},{6,5},{7,6},{8,7},{9,8},{10,9},{11,1... | collective-permute-start | bytes 2312 | tf_op jit(solution)/shard_map/while/body/eval_jaxpr/ppermute | solution.py:24
  626.8 18.7 %collective-permute-start.27 = (f32[6,1,32]{2,1,0:T(1,128)S(1)}, f32[6,1,32]{2,1,0:T(1,128)S(1)}, u32[]{:S(2)}, u32[]{:S(2)}) collective-permute-start(f32[6,1,32]{2,1,0:T(1,128)S(1)} %get-tuple-element.855), channel_id=1, source_target_pairs={{0,1},{1,2},{2,3},{3,4},{4,5},{5,6},{6,7},{7,8},{8,9},{9,10},{10,1... | collective-permute-start | bytes 2312 | tf_op jit(solution)/shard_map/while/body/eval_jaxpr/ppermute | solution.py:23
  687.9 7.2 collective-permute-start.35
  (197 other events, 802.1 us)
where the time goes:
time: 819 us; the launch traced here: 817 us
  waiting for transfers between devices  437 us (53%)
  starting transfers between devices  170 us (21%)
  local copies, waits for them, and re-layouts  107 us (13%)
  other arithmetic  51 us (6%)
  blocking collectives  44.7 us (5%)
    ppermute x114, waiting for transfers between devices, extended(): before = lax.ppermute(last, axis, up)  322 us
    ppermute x114, waiting for transfers between devices, extended(): after = lax.ppermute(leading, axis, down)  115 us
    ppermute x114, starting transfers between devices, extended(): before = lax.ppermute(last, axis, up)  115 us
    reshape x12, local copies, waits for them, and re-layouts, restrict(): blocks = field.reshape(size_x // 2, 2, size_y // 2, 2, size_z // 2, 2)  62.2 us
    ppermute x114, starting transfers between devices, extended(): after = lax.ppermute(leading, axis, down)  55.3 us
    psum x4, blocking collectives, one_axis_at_a_time(): x = lax.psum(x, axis)  44.7 us
    reduce_sum x18, other arithmetic, restrict(): return jnp.sum(blocks, axis=(1, 3, 5)) * 0.125  25.8 us
    reshape x9, local copies, waits for them, and re-layouts, prolong(): return spread.reshape(2 * size_x, 2 * size_y, 2 * size_z)  23 us
  transfers between devices with their start and end apart: 228, of which 198 were waited for; matrix products, arithmetic and copies ran while one was open for 13% of the time, Pallas kernels for 0%

commit v1 on v0

--- a/solution.py
+++ b/solution.py
@@ -11,6 +11,10 @@
 GY = ("gy_0", "gy_1")
 COUPLING = 0.1
 FLOOR = 3.0
+
+
+def sectors_expand(ax_name, inner_x):
+    return jnp.sum(lax.all_gather(inner_x, ax_name), axis=0)
 
 
 def extended(x, sides, width):
@@ -28,7 +32,7 @@
 
 def one_axis_at_a_time(x, axes):
     for axis in axes:
-        x = lax.psum(x, axis)
+        x = sectors_expand(axis, inner_x=x)
     return x
 
 

time: 819 us -> 829 us (1.012)
  local copies, waits for them, and re-layouts: 107 us -> 118 us
    psum x4 -> x0, blocking collectives: 44.7 us -> none  [one_axis_at_a_time(): x = lax.psum(x, axis)]
    unnamed x0 -> x4, blocking collectives: none -> 41.9 us
    unnamed x2 -> x14, local copies, waits for them, and re-layouts: 0.65 us -> 11.4 us
where the time goes in v1:
time: 829 us; the launch traced here: 827 us
  waiting for transfers between devices  437 us (53%)
  starting transfers between devices  170 us (21%)
  local copies, waits for them, and re-layouts  118 us (14%)
  other arithmetic  53.5 us (6%)
  blocking collectives  41.9 us (5%)
    ppermute x114, waiting for transfers between devices, extended(): before = lax.ppermute(last, axis, up)  322 us
    ppermute x114, waiting for transfers between devices, extended(): after = lax.ppermute(leading, axis, down)  115 us
    ppermute x114, starting transfers between devices, extended(): before = lax.ppermute(last, axis, up)  115 us
    reshape x12, local copies, waits for them, and re-layouts, restrict(): blocks = field.reshape(size_x // 2, 2, size_y // 2, 2, size_z // 2, 2)  62 us
    ppermute x114, starting transfers between devices, extended(): after = lax.ppermute(leading, axis, down)  55.3 us
    unnamed x4, blocking collectives  41.9 us
    reduce_sum x18, other arithmetic, restrict(): return jnp.sum(blocks, axis=(1, 3, 5)) * 0.125  25.6 us
    reshape x9, local copies, waits for them, and re-layouts, prolong(): return spread.reshape(2 * size_x, 2 * size_y, 2 * size_z)  23 us
  transfers between devices with their start and end apart: 228, of which 198 were waited for; matrix products, arithmetic and copies ran while one was open for 13% of the time, Pallas kernels for 0%

profile of v1, /device:TPU:0, one launch (start us, length us, event | category | flops | bytes accessed | tf_op | source)
XLA Modules:
  0.0 827.0 jit_solution(2199285411326393953)
XLA Ops:
  8.3 18.3 %all-reduce = f32[8]{0:T(128)S(1)} all-reduce(f32[8]{0:T(128)S(1)} %dynamic-update-slice), channel_id=1, replica_groups=mesh['gx_0'=8,'gx_1'=2,'gy_0'=4,'gy_1'=4] {'gx_0'}, use_global_device_ids=true, to_apply=%add | all-reduce | flops 8 | bytes 64
  33.1 10.5 %all-reduce.2 = f32[4]{0:T(128)S(1)} all-reduce(f32[4]{0:T(128)S(1)} %dynamic-update-slice.2), channel_id=1, replica_groups=mesh['gx_0'=8,'gx_1'=2,'gy_0'=4,'gy_1'=4] {'gy_0'}, use_global_device_ids=true, to_apply=%add.2 | all-reduce | flops 4 | bytes 32
  45.7 10.7 %all-reduce.3 = f32[4]{0:T(128)S(1)} all-reduce(f32[4]{0:T(128)S(1)} %dynamic-update-slice.3), channel_id=1, replica_groups=mesh['gx_0'=8,'gx_1'=2,'gy_0'=4,'gy_1'=4] {'gy_1'}, use_global_device_ids=true, to_apply=%add.3 | all-reduce | flops 4 | bytes 32
  58.8 767.1 %while.16 = (s32[]{:T(128)}, f32[16,16,128]{2,1,0:T(8,128)S(1)}, f32[16,16,128]{2,1,0:T(8,128)S(1)}, s32[16,16]{1,0:T(8,128)S(1)}, s32[8,8]{1,0:T(8,128)S(1)}, /...) while((s32[]{:T(128)}, f32[16,16,128]{2,1,0:T(8,128)S(1)}, ...), condition=%wide.region_12.13_spmd.clone.clone.clone, body=%wide.region_5.12_spmd.clone.clone.clone.sunk | while | flops 16104283 | bytes 31824424 | solution.py:229
  59.8 9.7 %reshape.277 = f32[8,2,8,2,64,2]{5,4,3,2,1,0:T(8,128)} reshape(f32[16,16,128]{2,1,0:T(8,128)S(1)} %broadcast_select_fusion.2) | data formatting | bytes 262144 | tf_op jit(solution)/shard_map/while/body/eval_jaxpr/reshape | solution.py:120
  69.6 4.0 reduce_sum.153
  86.1 5.4 collective-permute-start.39
  100.0 5.7 collective-permute-done.15
  105.8 4.2 collective-permute-done.5
  130.5 9.8 %reshape.276 = f32[8,2,8,2,64,2]{5,4,3,2,1,0:T(8,128)} reshape(f32[16,16,128]{2,1,0:T(8,128)S(1)} %fusion.546) | data formatting | bytes 262144 | tf_op jit(solution)/shard_map/while/body/eval_jaxpr/reshape | solution.py:120
  140.3 4.0 reduce_sum.152
  152.4 5.3 collective-permute-done.19
  278.6 4.0 broadcast_in_dim.60
  282.6 6.9 reshape.282
  315.0 9.7 %reshape.277 = f32[8,2,8,2,64,2]{5,4,3,2,1,0:T(8,128)} reshape(f32[16,16,128]{2,1,0:T(8,128)S(1)} %broadcast_select_fusion.2) | data formatting | bytes 262144 | tf_op jit(solution)/shard_map/while/body/eval_jaxpr/reshape | solution.py:120
  324.8 4.0 reduce_sum.153
  341.3 5.4 collective-permute-start.39
  355.2 5.7 collective-permute-done.15
  361.0 4.2 collective-permute-done.5
  386.0 9.8 %reshape.276 = f32[8,2,8,2,64,2]{5,4,3,2,1,0:T(8,128)} reshape(f32[16,16,128]{2,1,0:T(8,128)S(1)} %fusion.546) | data formatting | bytes 262144 | tf_op jit(solution)/shard_map/while/body/eval_jaxpr/reshape | solution.py:120
  395.7 4.0 reduce_sum.152
  407.9 5.3 collective-permute-done.19
  537.8 6.9 reshape.282
  570.5 9.7 %reshape.277 = f32[8,2,8,2,64,2]{5,4,3,2,1,0:T(8,128)} reshape(f32[16,16,128]{2,1,0:T(8,128)S(1)} %broadcast_select_fusion.2) | data formatting | bytes 262144 | tf_op jit(solution)/shard_map/while/body/eval_jaxpr/reshape | solution.py:120
  580.2 4.0 reduce_sum.153
  596.7 5.4 collective-permute-start.39
  610.7 5.7 collective-permute-done.15
  616.4 4.2 collective-permute-done.5
  641.2 9.8 %reshape.276 = f32[8,2,8,2,64,2]{5,4,3,2,1,0:T(8,128)} reshape(f32[16,16,128]{2,1,0:T(8,128)S(1)} %fusion.546) | data formatting | bytes 262144 | tf_op jit(solution)/shard_map/while/body/eval_jaxpr/reshape | solution.py:120
  650.9 4.0 reduce_sum.152
  663.1 5.3 collective-permute-done.19
  793.2 6.9 reshape.282
  (938 shorter events, 612.3 us)
Async XLA Ops:
  59.3 26.8 %collective-permute-start = (f32[1,16,128]{2,1,0:T(8,128)S(1)}, f32[1,16,128]{2,1,0:T(8,128)S(1)}, u32[]{:S(2)}, u32[]{:S(2)}) collective-permute-start(f32[1,16,128]{2,1,0:T(8,128)S(1)} %get-tuple-element.774), channel_id=1, source_target_pairs={{16,0},{32,16},{48,32},{64,48},{80,64},{96,80},{112,96},{128,112},... | collective-permute-start | bytes 24584 | tf_op jit(solution)/shard_map/while/body/eval_jaxpr/ppermute | solution.py:28
  59.3 32.2 %collective-permute-start.1 = (f32[1,16,128]{2,1,0:T(8,128)S(1)}, f32[1,16,128]{2,1,0:T(8,128)S(1)}, u32[]{:S(2)}, u32[]{:S(2)}) collective-permute-start(f32[1,16,128]{2,1,0:T(8,128)S(1)} %get-tuple-element.775), channel_id=1, source_target_pairs={{0,16},{16,32},{32,48},{48,64},{64,80},{80,96},{96,112},{112,128},... | collective-permute-start | bytes 24584 | tf_op jit(solution)/shard_map/while/body/eval_jaxpr/ppermute | solution.py:27
  73.6 18.0 %collective-permute-start.12 = (f32[1,8,64]{2,1,0:T(8,128)S(1)}, f32[1,8,64]{2,1,0:T(8,128)S(1)}, u32[]{:S(2)}, u32[]{:S(2)}) collective-permute-start(f32[1,8,64]{2,1,0:T(8,128)S(1)} %get-tuple-element.814), channel_id=1, source_target_pairs={{16,0},{32,16},{48,32},{64,48},{80,64},{96,80},{112,96},{128,112},... | collective-permute-start | bytes 6152 | tf_op jit(solution)/shard_map/while/body/eval_jaxpr/ppermute | solution.py:28
  83.1 8.6 %collective-permute-start.13 = (f32[1,8,64]{2,1,0:T(8,128)S(1)}, f32[1,8,64]{2,1,0:T(8,128)S(1)}, u32[]{:S(2)}, u32[]{:S(2)}) collective-permute-start(f32[1,8,64]{2,1,0:T(8,128)S(1)} %get-tuple-element.815), channel_id=1, source_target_pairs={{0,16},{16,32},{32,48},{48,64},{64,80},{80,96},{96,112},{112,128},... | collective-permute-start | bytes 6152 | tf_op jit(solution)/shard_map/while/body/eval_jaxpr/ppermute | solution.py:27
  86.1 85.8 %collective-permute-start.38 = (f32[4,1,16]{2,1,0:T(1,128)S(1)}, f32[4,1,16]{2,1,0:T(1,128)S(1)}, u32[]{:S(2)}, u32[]{:S(2)}) collective-permute-start(f32[4,1,16]{2,1,0:T(1,128)S(1)} %get-tuple-element.892), channel_id=1, source_target_pairs={{0,1},{1,2},{2,3},{3,4},{4,5},{5,6},{6,7},{7,8},{8,9},{9,10},{10,1... | collective-permute-start | bytes 776 | tf_op jit(solution)/shard_map/while/body/eval_jaxpr/ppermute | solution.py:27
  86.1 85.8 %collective-permute-start.39 = (f32[4,1,16]{2,1,0:T(1,128)S(1)}, f32[4,1,16]{2,1,0:T(1,128)S(1)}, u32[]{:S(2)}, u32[]{:S(2)}) collective-permute-start(f32[4,1,16]{2,1,0:T(1,128)S(1)} %get-tuple-element.893), channel_id=1, source_target_pairs={{1,0},{2,1},{3,2},{4,3},{5,4},{6,5},{7,6},{8,7},{9,8},{10,9},{11,1... | collective-permute-start | bytes 776 | tf_op jit(solution)/shard_map/while/body/eval_jaxpr/ppermute | solution.py:28
  91.5 53.0 %collective-permute-start.26 = (f32[6,1,32]{2,1,0:T(1,128)S(1)}, f32[6,1,32]{2,1,0:T(1,128)S(1)}, u32[]{:S(2)}, u32[]{:S(2)}) collective-permute-start(f32[6,1,32]{2,1,0:T(1,128)S(1)} %get-tuple-element.854), channel_id=1, source_target_pairs={{1,0},{2,1},{3,2},{4,3},{5,4},{6,5},{7,6},{8,7},{9,8},{10,9},{11,1... | collective-permute-start | bytes 2312 | tf_op jit(solution)/shard_map/while/body/eval_jaxpr/ppermute | solution.py:28
  91.7 7.1 collective-permute-start.3
  126.3 18.6 %collective-permute-start.27 = (f32[6,1,32]{2,1,0:T(1,128)S(1)}, f32[6,1,32]{2,1,0:T(1,128)S(1)}, u32[]{:S(2)}, u32[]{:S(2)}) collective-permute-start(f32[6,1,32]{2,1,0:T(1,128)S(1)} %get-tuple-element.855), channel_id=1, source_target_pairs={{0,1},{1,2},{2,3},{3,4},{4,5},{5,6},{6,7},{7,8},{8,9},{9,10},{10,1... | collective-permute-start | bytes 2312 | tf_op jit(solution)/shard_map/while/body/eval_jaxpr/ppermute | solution.py:27
  187.4 7.2 collective-permute-start.35
  294.0 7.1 collective-permute-start.71
  306.3 7.1 collective-permute-start.75
  314.5 26.8 %collective-permute-start = (f32[1,16,128]{2,1,0:T(8,128)S(1)}, f32[1,16,128]{2,1,0:T(8,128)S(1)}, u32[]{:S(2)}, u32[]{:S(2)}) collective-permute-start(f32[1,16,128]{2,1,0:T(8,128)S(1)} %get-tuple-element.774), channel_id=1, source_target_pairs={{16,0},{32,16},{48,32},{64,48},{80,64},{96,80},{112,96},{128,112},... | collective-permute-start | bytes 24584 | tf_op jit(solution)/shard_map/while/body/eval_jaxpr/ppermute | solution.py:28
  314.5 32.2 %collective-permute-start.1 = (f32[1,16,128]{2,1,0:T(8,128)S(1)}, f32[1,16,128]{2,1,0:T(8,128)S(1)}, u32[]{:S(2)}, u32[]{:S(2)}) collective-permute-start(f32[1,16,128]{2,1,0:T(8,128)S(1)} %get-tuple-element.775), channel_id=1, source_target_pairs={{0,16},{16,32},{32,48},{48,64},{64,80},{80,96},{96,112},{112,128},... | collective-permute-start | bytes 24584 | tf_op jit(solution)/shard_map/while/body/eval_jaxpr/ppermute | solution.py:27
  328.8 18.0 %collective-permute-start.12 = (f32[1,8,64]{2,1,0:T(8,128)S(1)}, f32[1,8,64]{2,1,0:T(8,128)S(1)}, u32[]{:S(2)}, u32[]{:S(2)}) collective-permute-start(f32[1,8,64]{2,1,0:T(8,128)S(1)} %get-tuple-element.814), channel_id=1, source_target_pairs={{16,0},{32,16},{48,32},{64,48},{80,64},{96,80},{112,96},{128,112},... | collective-permute-start | bytes 6152 | tf_op jit(solution)/shard_map/while/body/eval_jaxpr/ppermute | solution.py:28
  338.3 8.6 %collective-permute-start.13 = (f32[1,8,64]{2,1,0:T(8,128)S(1)}, f32[1,8,64]{2,1,0:T(8,128)S(1)}, u32[]{:S(2)}, u32[]{:S(2)}) collective-permute-start(f32[1,8,64]{2,1,0:T(8,128)S(1)} %get-tuple-element.815), channel_id=1, source_target_pairs={{0,16},{16,32},{32,48},{48,64},{64,80},{80,96},{96,112},{112,128},... | collective-permute-start | bytes 6152 | tf_op jit(solution)/shard_map/while/body/eval_jaxpr/ppermute | solution.py:27
  341.3 86.0 %collective-permute-start.38 = (f32[4,1,16]{2,1,0:T(1,128)S(1)}, f32[4,1,16]{2,1,0:T(1,128)S(1)}, u32[]{:S(2)}, u32[]{:S(2)}) collective-permute-start(f32[4,1,16]{2,1,0:T(1,128)S(1)} %get-tuple-element.892), channel_id=1, source_target_pairs={{0,1},{1,2},{2,3},{3,4},{4,5},{5,6},{6,7},{7,8},{8,9},{9,10},{10,1... | collective-permute-start | bytes 776 | tf_op jit(solution)/shard_map/while/body/eval_jaxpr/ppermute | solution.py:27
  341.3 86.0 %collective-permute-start.39 = (f32[4,1,16]{2,1,0:T(1,128)S(1)}, f32[4,1,16]{2,1,0:T(1,128)S(1)}, u32[]{:S(2)}, u32[]{:S(2)}) collective-permute-start(f32[4,1,16]{2,1,0:T(1,128)S(1)} %get-tuple-element.893), channel_id=1, source_target_pairs={{1,0},{2,1},{3,2},{4,3},{5,4},{6,5},{7,6},{8,7},{9,8},{10,9},{11,1... | collective-permute-start | bytes 776 | tf_op jit(solution)/shard_map/while/body/eval_jaxpr/ppermute | solution.py:28
  346.7 53.2 %collective-permute-start.26 = (f32[6,1,32]{2,1,0:T(1,128)S(1)}, f32[6,1,32]{2,1,0:T(1,128)S(1)}, u32[]{:S(2)}, u32[]{:S(2)}) collective-permute-start(f32[6,1,32]{2,1,0:T(1,128)S(1)} %get-tuple-element.854), channel_id=1, source_target_pairs={{1,0},{2,1},{3,2},{4,3},{5,4},{6,5},{7,6},{8,7},{9,8},{10,9},{11,1... | collective-permute-start | bytes 2312 | tf_op jit(solution)/shard_map/while/body/eval_jaxpr/ppermute | solution.py:28
  365.3 7.1 collective-permute-start.7
  378.1 7.1 collective-permute-start.11
  381.8 18.6 %collective-permute-start.27 = (f32[6,1,32]{2,1,0:T(1,128)S(1)}, f32[6,1,32]{2,1,0:T(1,128)S(1)}, u32[]{:S(2)}, u32[]{:S(2)}) collective-permute-start(f32[6,1,32]{2,1,0:T(1,128)S(1)} %get-tuple-element.855), channel_id=1, source_target_pairs={{0,1},{1,2},{2,3},{3,4},{4,5},{5,6},{6,7},{7,8},{8,9},{9,10},{10,1... | collective-permute-start | bytes 2312 | tf_op jit(solution)/shard_map/while/body/eval_jaxpr/ppermute | solution.py:27
  442.8 7.2 collective-permute-start.35
  569.9 26.8 %collective-permute-start = (f32[1,16,128]{2,1,0:T(8,128)S(1)}, f32[1,16,128]{2,1,0:T(8,128)S(1)}, u32[]{:S(2)}, u32[]{:S(2)}) collective-permute-start(f32[1,16,128]{2,1,0:T(8,128)S(1)} %get-tuple-element.774), channel_id=1, source_target_pairs={{16,0},{32,16},{48,32},{64,48},{80,64},{96,80},{112,96},{128,112},... | collective-permute-start | bytes 24584 | tf_op jit(solution)/shard_map/while/body/eval_jaxpr/ppermute | solution.py:28
  570.0 32.2 %collective-permute-start.1 = (f32[1,16,128]{2,1,0:T(8,128)S(1)}, f32[1,16,128]{2,1,0:T(8,128)S(1)}, u32[]{:S(2)}, u32[]{:S(2)}) collective-permute-start(f32[1,16,128]{2,1,0:T(8,128)S(1)} %get-tuple-element.775), channel_id=1, source_target_pairs={{0,16},{16,32},{32,48},{48,64},{64,80},{80,96},{96,112},{112,128},... | collective-permute-start | bytes 24584 | tf_op jit(solution)/shard_map/while/body/eval_jaxpr/ppermute | solution.py:27
  584.2 18.0 %collective-permute-start.12 = (f32[1,8,64]{2,1,0:T(8,128)S(1)}, f32[1,8,64]{2,1,0:T(8,128)S(1)}, u32[]{:S(2)}, u32[]{:S(2)}) collective-permute-start(f32[1,8,64]{2,1,0:T(8,128)S(1)} %get-tuple-element.814), channel_id=1, source_target_pairs={{16,0},{32,16},{48,32},{64,48},{80,64},{96,80},{112,96},{128,112},... | collective-permute-start | bytes 6152 | tf_op jit(solution)/shard_map/while/body/eval_jaxpr/ppermute | solution.py:28
  593.8 8.6 %collective-permute-start.13 = (f32[1,8,64]{2,1,0:T(8,128)S(1)}, f32[1,8,64]{2,1,0:T(8,128)S(1)}, u32[]{:S(2)}, u32[]{:S(2)}) collective-permute-start(f32[1,8,64]{2,1,0:T(8,128)S(1)} %get-tuple-element.815), channel_id=1, source_target_pairs={{0,16},{16,32},{32,48},{48,64},{64,80},{80,96},{96,112},{112,128},... | collective-permute-start | bytes 6152 | tf_op jit(solution)/shard_map/while/body/eval_jaxpr/ppermute | solution.py:27
  596.7 85.8 %collective-permute-start.38 = (f32[4,1,16]{2,1,0:T(1,128)S(1)}, f32[4,1,16]{2,1,0:T(1,128)S(1)}, u32[]{:S(2)}, u32[]{:S(2)}) collective-permute-start(f32[4,1,16]{2,1,0:T(1,128)S(1)} %get-tuple-element.892), channel_id=1, source_target_pairs={{0,1},{1,2},{2,3},{3,4},{4,5},{5,6},{6,7},{7,8},{8,9},{9,10},{10,1... | collective-permute-start | bytes 776 | tf_op jit(solution)/shard_map/while/body/eval_jaxpr/ppermute | solution.py:27
  596.7 85.8 %collective-permute-start.39 = (f32[4,1,16]{2,1,0:T(1,128)S(1)}, f32[4,1,16]{2,1,0:T(1,128)S(1)}, u32[]{:S(2)}, u32[]{:S(2)}) collective-permute-start(f32[4,1,16]{2,1,0:T(1,128)S(1)} %get-tuple-element.893), channel_id=1, source_target_pairs={{1,0},{2,1},{3,2},{4,3},{5,4},{6,5},{7,6},{8,7},{9,8},{10,9},{11,1... | collective-permute-start | bytes 776 | tf_op jit(solution)/shard_map/while/body/eval_jaxpr/ppermute | solution.py:28
  602.1 53.0 %collective-permute-start.26 = (f32[6,1,32]{2,1,0:T(1,128)S(1)}, f32[6,1,32]{2,1,0:T(1,128)S(1)}, u32[]{:S(2)}, u32[]{:S(2)}) collective-permute-start(f32[6,1,32]{2,1,0:T(1,128)S(1)} %get-tuple-element.854), channel_id=1, source_target_pairs={{1,0},{2,1},{3,2},{4,3},{5,4},{6,5},{7,6},{8,7},{9,8},{10,9},{11,1... | collective-permute-start | bytes 2312 | tf_op jit(solution)/shard_map/while/body/eval_jaxpr/ppermute | solution.py:28
  637.0 18.6 %collective-permute-start.27 = (f32[6,1,32]{2,1,0:T(1,128)S(1)}, f32[6,1,32]{2,1,0:T(1,128)S(1)}, u32[]{:S(2)}, u32[]{:S(2)}) collective-permute-start(f32[6,1,32]{2,1,0:T(1,128)S(1)} %get-tuple-element.855), channel_id=1, source_target_pairs={{0,1},{1,2},{2,3},{3,4},{4,5},{5,6},{6,7},{7,8},{8,9},{9,10},{10,1... | collective-permute-start | bytes 2312 | tf_op jit(solution)/shard_map/while/body/eval_jaxpr/ppermute | solution.py:27
  698.0 7.2 collective-permute-start.35
  (197 other events, 802.1 us)
